TPU v7x, 256 devices: a whole 4x4x8 slice. The times are simulated.
256 devices in a mesh: row: 8 (over y, core), col: 32 (over x, z).
Axes of the slice: x: 4, y: 4, z: 8, core: 2. Of those that a mesh axis runs over, the one named last changes fastest.
Arguments:
- adjacency: int32 [27136, 27136], P('row', 'col'), may hold values from 0 to 3
- degree: int32 [27136], replicated, may hold values from 64 to 511
- cotangent: bfloat16 [27136, 512], P(('row', 'col')), may hold values from -6 to 6
- features: bfloat16 [27136, 512], P('col'), may hold values from -0.029907227 to 0.029907227
- weight: bfloat16 [512, 512], replicated, may hold values from -0.25 to 0.25
Outputs:
- grad_input: bfloat16 [27136, 512], P('col', 'row')
- grad_weight: float32 [512, 512], P('col', 'row')
All inputs are finite; a program needn't handle non-finite values.
Results may differ from a plain program's by a relative error of at most 0.0058.
Values may be sent and summed in bfloat16 or wider, within the bound.
No kernel may reach another device: no remote copies, remote signals or barrier semaphores. Data moves between devices by JAX's collectives and lax.ppermute only.
A program may use at most 128 MiB of HBM per device.

v0:
```python
import jax
import jax.numpy as jnp
from jax import lax
from jax.sharding import Mesh
from jax.sharding import PartitionSpec as P

COL = ("col_0", "col_1")
ROW_COL = ("row", "col_0", "col_1")


def laid_out(blocks, dim):
    lengths = list(blocks.shape[1:])
    lengths[dim] *= blocks.shape[0]
    return jnp.moveaxis(blocks, 0, dim).reshape(lengths)


def gather_in_order(value, axes, turns):
    blocks = value[None]
    for k in turns:
        blocks = lax.all_gather(blocks, axes[k], axis=0, tiled=True)
    current = [lax.axis_size(axes[k]) for k in reversed(turns)]
    blocks = blocks.reshape(*current, *value.shape)
    turned = sorted(range(len(turns)), key=lambda place: turns[len(turns) - 1 - place])
    return blocks.transpose(*turned, *range(len(turns), blocks.ndim)).reshape(-1, *value.shape)


def gather_axes(value, axes, turns, dim):
    return laid_out(gather_in_order(value, axes, turns), dim)


def split_up(value, dim, length):
    lengths = value.shape
    blocks = value.reshape(*lengths[:dim], length, lengths[dim] // length, *lengths[dim + 1 :])
    return jnp.moveaxis(blocks, dim, 0)


def summed_on_arrival(value, axis, dim):
    blocks = split_up(value, dim, lax.axis_size(axis))
    arrived = lax.all_to_all(blocks, axis, split_axis=0, concat_axis=0, tiled=True)
    return arrived.sum(axis=0)


def copy_for_each(value, axis):
    copies = jnp.broadcast_to(value, (lax.axis_size(axis), *value.shape))
    return lax.all_to_all(copies, axis, split_axis=0, concat_axis=0, tiled=True)


def collect(value, axis, dim):
    return laid_out(copy_for_each(value, axis), dim)


def per_device(adjacency, degree, cotangent, features, weight):
    rows_here, cols_here = adjacency.shape
    row_index = lax.axis_index("row")
    col_index = lax.axis_index(COL)
    inv_root = lax.rsqrt(degree.astype(jnp.float32))
    row_scale = lax.dynamic_slice_in_dim(inv_root, row_index * rows_here, rows_here, 0)
    col_scale = lax.dynamic_slice_in_dim(inv_root, col_index * cols_here, cols_here, 0)
    tile = adjacency.astype(jnp.bfloat16)
    width = weight.shape[0]
    scaled = (
        gather_axes(cotangent, COL, (0, 1), 0).astype(jnp.float32) * row_scale[:, None]
    ).astype(jnp.bfloat16)
    partial_sum = lax.dot_general(
        tile, scaled, (((0,), (0,)), ((), ())), preferred_element_type=jnp.float32
    )
    share = width // lax.axis_size("row")
    weight_rows = lax.dynamic_slice_in_dim(weight, row_index * share, share, 0)
    pieces = summed_on_arrival(partial_sum, "row", 1)
    z_columns = (pieces * col_scale[:, None]).astype(jnp.bfloat16)
    grad_z = collect(z_columns, "row", 1)
    grad_input = lax.dot_general(
        grad_z, weight_rows, (((1,), (1,)), ((), ())), preferred_element_type=jnp.float32
    )
    weight_term = lax.dot_general(
        features, z_columns, (((0,), (0,)), ((), ())), preferred_element_type=jnp.float32
    )
    grad_weight = summed_on_arrival(weight_term, COL, 0)
    return (grad_input.astype(jnp.bfloat16), grad_weight)


def solution(mesh):
    torus = Mesh(mesh.devices.reshape(mesh.shape["row"], 4, 8), ("row", "col_0", "col_1"))
    placed = (P("row", COL), P(), P(ROW_COL, None), P(COL, None), P())
    return jax.shard_map(
        per_device,
        mesh=torus,
        in_specs=placed,
        out_specs=(P(COL, "row"), P(COL, "row")),
        check_vma=False,
    )
```

profile of v0, /device:TPU:1, one launch (start us, length us, event | category | flops | bytes accessed | tf_op | source)
XLA Modules:
  0.0 172.6 jit_solution(2381927909333478503)
XLA Ops:
  7.2 0.0 copy-start
  7.2 0.0 all-gather.4.cloned.1.call-start
  7.2 13.1 %all-gather.1 = bf16[4,106,512]{2,1,0:T(8,128)(2,1)} all-gather(bf16[1,106,512]{2,1,0:T(8,128)(2,1)} %bitcast.23), channel_id=2, replica_groups=mesh['row'=8,'col_0'=4,'col_1'=8] {'col_0'}, dimensions={0}, use_global_device_ids=true | all-gather | bytes 542720 | tf_op jit(solution)/shard_map/all_gather | solution.py:20
  20.3 0.0 all-gather.4.cloned.1.call-update
  20.4 0.9 convert_rsqrt_fusion
  21.3 0.1 dynamic_slice.9
  21.4 53.0 %all-gather.4.cloned.1.call-done = bf16[32,106,512]{2,1,0:T(8,128)(2,1)} async-done(((bf16[4,106,512]{2,1,0:T(8,128)(2,1)}), bf16[32,106,512]{2,1,0:T(8,128)(2,1)}) %all-gather.4.cloned.1.call-update) | async-done | bytes 3473424 | tf_op jit(solution)/shard_map/all_gather | solution.py:20
  74.3 6.1 %copy_bitcast_fusion = f32[4,8,106,512]{3,2,1,0:T(8,128)} fusion(bf16[8,4,106,512]{3,2,1,0:T(8,128)(2,1)} %bitcast.21), kind=kLoop, calls=%fused_computation | loop fusion | flops 1736704 | bytes 10420224 | tf_op jit(solution)/shard_map/convert_element_type | solution.py:62
  80.4 6.6 %reshape.23 = f32[3392,512]{1,0:T(8,128)} reshape(f32[4,8,106,512]{3,2,1,0:T(8,128)} %copy_bitcast_fusion) | data formatting | bytes 13893632 | tf_op jit(solution)/shard_map/convert_element_type | solution.py:62
  87.0 9.7 %fusion.3 = f32[848,512]{1,0:T(8,128)S(1)} fusion(f32[3392,512]{1,0:T(8,128)} %reshape.23, f32[3392]{0:T(1024)S(1)} %dynamic_slice.9, s32[3392,848]{0,1:T(8,128)} %param.5), kind=kOutput, calls=%fused_computation.5 | convolution fusion | flops 2951799808 | bytes 20202752 | tf_op jit(solution)/shard_map/dot_general | solution.py:64
  96.7 1.7 copy.11
  98.4 5.1 %all-to-all-start = ((f32[8,848,64]{1,2,0:T(8,128)}), f32[8,848,64]{1,2,0:T(8,128)S(1)}, u32[]{:S(2)}, u32[]{:S(2)}) async-start(f32[8,848,64]{1,2,0:T(8,128)} %bitcast.19), calls=%async_computation | async-start | bytes 3670016 | tf_op jit(solution)/shard_map/all_to_all | solution.py:39
  103.5 0.1 dynamic_slice.10
  103.6 23.3 %all-to-all-done = f32[8,848,64]{1,2,0:T(8,128)S(1)} async-done(((f32[8,848,64]{1,2,0:T(8,128)}), f32[8,848,64]{1,2,0:T(8,128)S(1)}, u32[]{:S(2)}, u32[]{:S(2)}) %all-to-all-start) | async-done | bytes 1736736 | tf_op jit(solution)/shard_map/all_to_all | solution.py:39
  126.9 0.1 reduce_sum.18
  127.0 0.0 copy-done
  127.0 0.3 convolution_bitcast_fusion
  127.3 0.1 copy.12
  127.5 0.2 reshape.29
  127.7 15.8 %all_to_all.15 = f32[32,1,1024]{2,1,0:T(1,128)S(1)} all-to-all(f32[32,1,1024]{2,1,0:T(1,128)S(1)} %reshape.29), channel_id=1, replica_groups=mesh['row'=8,'col_0'=4,'col_1'=8] {'col_0','col_1'}, dimensions={0} | all-to-all | bytes 262144 | tf_op jit(solution)/shard_map/all_to_all | solution.py:39
  143.5 1.0 broadcast_in_dim.9
  144.5 5.8 %all-to-all-start.1 = ((bf16[8,848,64]{1,2,0:T(8,128)(2,1)}), bf16[8,848,64]{1,2,0:T(8,128)(2,1)S(1)}, u32[]{:S(2)}, u32[]{:S(2)}) async-start(bf16[8,848,64]{1,2,0:T(8,128)(2,1)} %broadcast_in_dim.9), calls=%async_computation.1 | async-start | bytes 1835008 | tf_op jit(solution)/shard_map/all_to_all | solution.py:45
  150.3 0.5 broadcast.2
  150.9 0.9 reduce
  151.8 0.1 reshape.30
  151.9 0.6 reduce_sum.19
  152.6 11.4 %all-to-all-done.1 = bf16[8,848,64]{1,2,0:T(8,128)(2,1)S(1)} async-done(((bf16[8,848,64]{1,2,0:T(8,128)(2,1)}), bf16[8,848,64]{1,2,0:T(8,128)(2,1)S(1)}, u32[]{:S(2)}, u32[]{:S(2)}) %all-to-all-start.1) | async-done | bytes 868384 | tf_op jit(solution)/shard_map/all_to_all | solution.py:45
  163.9 1.8 %convolution_convert_fusion = bf16[848,64]{0,1:T(8,128)(2,1)} fusion(bf16[848,512]{0,1:T(8,128)(2,1)S(1)} %bitcast.20, bf16[512,512]{1,0:T(8,128)(2,1)} %param.9, s32[]{:T(128)S(6)} %select_n.11), kind=kOutput, calls=%fused_computation.6 | convolution fusion | flops 55628800 | bytes 1042436 | tf_op jit(solution)/shard_map/dot_general | solution.py:72
  (1 shorter events, 0.0 us)
Async XLA Ops:
  7.2 119.9 %copy-start = (bf16[848,512]{1,0:T(8,128)(2,1)S(1)}, bf16[848,512]{1,0:T(8,128)(2,1)}, u32[]{:S(2)}) copy-start(bf16[848,512]{1,0:T(8,128)(2,1)} %param.8) | copy-start | bytes 2605060
  7.2 67.2 %all-gather.4.cloned.1.call-start = ((), (), s32[]{:S(2)}) async-start(), calls=%async_computation.3 | async-start | bytes 4128768 | tf_op jit(solution)/shard_map/all_gather | solution.py:20
  98.4 28.5 %all-to-all-start = ((f32[8,848,64]{1,2,0:T(8,128)}), f32[8,848,64]{1,2,0:T(8,128)S(1)}, u32[]{:S(2)}, u32[]{:S(2)}) async-start(f32[8,848,64]{1,2,0:T(8,128)} %bitcast.19), calls=%async_computation | async-start | bytes 3670016 | tf_op jit(solution)/shard_map/all_to_all | solution.py:39
  144.5 19.4 %all-to-all-start.1 = ((bf16[8,848,64]{1,2,0:T(8,128)(2,1)}), bf16[8,848,64]{1,2,0:T(8,128)(2,1)S(1)}, u32[]{:S(2)}, u32[]{:S(2)}) async-start(bf16[8,848,64]{1,2,0:T(8,128)(2,1)} %broadcast_in_dim.9), calls=%async_computation.1 | async-start | bytes 1835008 | tf_op jit(solution)/shard_map/all_to_all | solution.py:45
Sparse Core Ops, SparseCore 0:
  20.5 53.8 all-gather.3
where the time goes:
time: 173 us
  waiting for transfers between devices  87.7 us (51%)
  blocking collectives  28.9 us (17%)
  between operations  14.1 us (8%)
  matrix products  11.7 us (7%)
  starting transfers between devices  11 us (6%)
  local copies, waits for them, and re-layouts  10.5 us (6%)
  other arithmetic  8.69 us (5%)
    all_gather x1, waiting for transfers between devices, gather_in_order(): blocks = lax.all_gather(blocks, axes[k], axis=0, tiled=True)  53 us
    all_to_all x1, waiting for transfers between devices, summed_on_arrival(): lax.all_to_all(blocks, axis, split_axis=0, concat_axis=0, tiled=True)  23.3 us
    all_to_all x1, blocking collectives, summed_on_arrival(): lax.all_to_all(blocks, axis, split_axis=0, concat_axis=0, tiled=True)  15.8 us
    all_gather x1, blocking collectives, gather_in_order(): blocks = lax.all_gather(blocks, axes[k], axis=0, tiled=True)  13.1 us
    all_to_all x1, waiting for transfers between devices, copy_for_each(): return lax.all_to_all(copies, axis, split_axis=0, concat_axis=0, tiled=True)  11.4 us
    dot_general x1, matrix products, per_device(): lax.dot_general(tile, scaled, (((0,), (0,)), ((), ())), preferred_element...  9.67 us
    convert_element_type x1, local copies, waits for them, and re-layouts, per_device(): gather_axes(cotangent, COL, (0, 1), 0).astype(jnp.float32)  6.6 us
    convert_element_type x1, other arithmetic, per_device(): gather_axes(cotangent, COL, (0, 1), 0).astype(jnp.float32)  6.06 us
  transfers between devices with their start and end apart: 3, of which 3 were waited for; matrix products, arithmetic and copies ran while one was open for 2% of the time, Pallas kernels for 0%

commit v1 on v0

--- a/solution.py
+++ b/solution.py
@@ -17,7 +17,9 @@
 def gather_in_order(value, axes, turns):
     blocks = value[None]
     for k in turns:
-        blocks = lax.all_gather(blocks, axes[k], axis=0, tiled=True)
+        blocks = jnp.concatenate(
+            lax.all_to_all(jnp.stack([blocks] * lax.axis_size(axes[k])), axes[k], 0, 0), axis=0
+        )
     current = [lax.axis_size(axes[k]) for k in reversed(turns)]
     blocks = blocks.reshape(*current, *value.shape)
     turned = sorted(range(len(turns)), key=lambda place: turns[len(turns) - 1 - place])

time: 173 us -> 197 us (1.14)
  waiting for transfers between devices: 87.7 us -> 116 us
  between operations: 14.1 us -> 0.73 us
  local copies, waits for them, and re-layouts: 10.5 us -> 19.6 us
  starting transfers between devices: 11 us -> 18.7 us
  blocking collectives: 28.9 us -> 24.4 us
  other arithmetic: 8.69 us -> 5.05 us
    all_to_all x0 -> x1, waiting for transfers between devices: none -> 81.2 us  [gather_in_order(): lax.all_to_all(jnp.stack([blocks] * lax.axis_size(axes[k])), axes[k], 0, 0)]
    all_gather x1 -> x0, waiting for transfers between devices: 53 us -> none  [gather_in_order(): blocks = lax.all_gather(blocks, axes[k], axis=0, tiled=True)]
    all_gather x1 -> x0, blocking collectives: 13.1 us -> none  [gather_in_order(): blocks = lax.all_gather(blocks, axes[k], axis=0, tiled=True)]
    all_to_all x0 -> x1, blocking collectives: none -> 12.3 us  [gather_in_order(): lax.all_to_all(jnp.stack([blocks] * lax.axis_size(axes[k])), axes[k], 0, 0)]
    all_to_all x0 -> x1, starting transfers between devices: none -> 8.19 us  [gather_in_order(): lax.all_to_all(jnp.stack([blocks] * lax.axis_size(axes[k])), axes[k], 0, 0)]
    convert_element_type x1 -> x2, local copies, waits for them, and re-layouts: 6.6 us -> 11.7 us  [per_device(): gather_axes(cotangent, COL, (0, 1), 0).astype(jnp.float32)]
    another operation x0 -> x3, local copies, waits for them, and re-layouts: none -> 4.06 us  [gather_in_order(): jnp.stack([blocks] * lax.axis_size(axes[k]))]
    all_to_all x1, blocking collectives: 15.8 us -> 12.1 us  [summed_on_arrival(): lax.all_to_all(blocks, axis, split_axis=0, concat_axis=0, tiled=True)]
  transfers between devices with their start and end apart: 3 -> 3, of which waited for: 3 -> 3; matrix products, arithmetic and copies ran while one was open for 2% -> 1% of each run, Pallas kernels for 0% -> 0%
where the time goes in v1:
time: 197 us; the launch traced here: 196 us
  waiting for transfers between devices  116 us (59%)
  blocking collectives  24.4 us (12%)
  local copies, waits for them, and re-layouts  19.6 us (10%)
  starting transfers between devices  18.7 us (9%)
  matrix products  11.7 us (6%)
  other arithmetic  5.05 us (3%)
    all_to_all x1, waiting for transfers between devices, gather_in_order(): lax.all_to_all(jnp.stack([blocks] * lax.axis_size(axes[k])), axes[k], 0, 0)  81.2 us
    all_to_all x1, waiting for transfers between devices, summed_on_arrival(): lax.all_to_all(blocks, axis, split_axis=0, concat_axis=0, tiled=True)  23.3 us
    all_to_all x1, blocking collectives, gather_in_order(): lax.all_to_all(jnp.stack([blocks] * lax.axis_size(axes[k])), axes[k], 0, 0)  12.3 us
    all_to_all x1, blocking collectives, summed_on_arrival(): lax.all_to_all(blocks, axis, split_axis=0, concat_axis=0, tiled=True)  12.1 us
    convert_element_type x2, local copies, waits for them, and re-layouts, per_device(): gather_axes(cotangent, COL, (0, 1), 0).astype(jnp.float32)  11.7 us
    all_to_all x1, waiting for transfers between devices, copy_for_each(): return lax.all_to_all(copies, axis, split_axis=0, concat_axis=0, tiled=True)  11.4 us
    dot_general x1, matrix products, per_device(): lax.dot_general(tile, scaled, (((0,), (0,)), ((), ())), preferred_element...  9.68 us
    all_to_all x1, starting transfers between devices, gather_in_order(): lax.all_to_all(jnp.stack([blocks] * lax.axis_size(axes[k])), axes[k], 0, 0)  8.19 us
  transfers between devices with their start and end apart: 3, of which 3 were waited for; matrix products, arithmetic and copies ran while one was open for 1% of the time, Pallas kernels for 0%

profile of v1, /device:TPU:1, one launch (start us, length us, event | category | flops | bytes accessed | tf_op | source)
XLA Modules:
  0.0 196.1 jit_solution(8359455302871700676)
XLA Ops:
  0.6 0.0 copy-start
  0.6 0.0 copy-start.1
  0.7 1.0 stack.6
  1.7 12.3 %all_to_all.25 = bf16[4,1,106,512]{3,2,1,0:T(8,128)(2,1)S(1)} all-to-all(bf16[4,1,106,512]{3,2,1,0:T(8,128)(2,1)S(1)} %stack.6), channel_id=1, replica_groups=mesh['row'=8,'col_0'=4,'col_1'=8] {'col_0'}, dimensions={0} | all-to-all | bytes 868352 | tf_op jit(solution)/shard_map/all_to_all | solution.py:21
  13.9 0.3 copy.9
  14.3 2.7 %stack.7 = bf16[8,4,106,512]{3,1,2,0:T(4,128)(2,1)} broadcast(bf16[4,106,512]{2,0,1:T(4,128)(2,1)S(1)} %copy.9), dimensions={1,2,3} | broadcast | bytes 3907584 | tf_op jit(solution)/shard_map/stack | solution.py:21
  17.0 8.2 %all-to-all-start.1 = ((bf16[8,4,106,512]{3,1,2,0:T(4,128)(2,1)}), bf16[8,4,106,512]{3,1,2,0:T(4,128)(2,1)}, u32[]{:S(2)}, u32[]{:S(2)}) async-start(bf16[8,4,106,512]{3,1,2,0:T(4,128)(2,1)} %stack.7), calls=%async_computation.1 | async-start | bytes 6946816 | tf_op jit(solution)/shard_map/all_to_all | solution.py:21
  25.2 0.0 copy-done.1
  25.2 0.1 dynamic_slice.9
  25.3 81.2 %all-to-all-done.1 = bf16[8,4,106,512]{3,1,2,0:T(4,128)(2,1)} async-done(((bf16[8,4,106,512]{3,1,2,0:T(4,128)(2,1)}), bf16[8,4,106,512]{3,1,2,0:T(4,128)(2,1)}, u32[]{:S(2)}, u32[]{:S(2)}) %all-to-all-start.1) | async-done | bytes 3473440 | tf_op jit(solution)/shard_map/all_to_all | solution.py:21
  106.5 3.3 %convert_bitcast_fusion = f32[4,8,106,512]{3,0,2,1:T(4,128)S(1)} fusion(bf16[8,4,106,512]{3,1,2,0:T(4,128)(2,1)} %all-to-all-done.1), kind=kLoop, calls=%fused_computation | loop fusion | flops 1736704 | bytes 10420224 | tf_op jit(solution)/shard_map/convert_element_type | solution.py:64
  109.8 5.1 %copy.10 = f32[4,8,106,512]{3,2,1,0:T(8,128)} copy(f32[4,8,106,512]{3,0,2,1:T(4,128)S(1)} %convert_bitcast_fusion) | data formatting | bytes 13893632 | tf_op jit(solution)/shard_map/convert_element_type | solution.py:64
  114.9 6.6 %reshape.24 = f32[3392,512]{1,0:T(8,128)} reshape(f32[4,8,106,512]{3,2,1,0:T(8,128)} %copy.10) | data formatting | bytes 13893632 | tf_op jit(solution)/shard_map/convert_element_type | solution.py:64
  121.5 9.7 %fusion.3 = f32[848,512]{1,0:T(8,128)S(1)} fusion(f32[3392,512]{1,0:T(8,128)} %reshape.24, f32[3392]{0:T(1024)S(1)} %dynamic_slice.9, s32[3392,848]{0,1:T(8,128)} %param.5), kind=kOutput, calls=%fused_computation.5 | convolution fusion | flops 2951799808 | bytes 20202752 | tf_op jit(solution)/shard_map/dot_general | solution.py:66
  131.2 1.7 copy.11
  132.9 4.9 %all-to-all-start.2 = ((f32[8,848,64]{1,2,0:T(8,128)}), f32[8,848,64]{1,2,0:T(8,128)S(1)}, u32[]{:S(2)}, u32[]{:S(2)}) async-start(f32[8,848,64]{1,2,0:T(8,128)} %bitcast.17), calls=%async_computation.2 | async-start | bytes 3670016 | tf_op jit(solution)/shard_map/all_to_all | solution.py:41
  137.9 0.1 dynamic_slice.10
  138.0 23.3 %all-to-all-done.2 = f32[8,848,64]{1,2,0:T(8,128)S(1)} async-done(((f32[8,848,64]{1,2,0:T(8,128)}), f32[8,848,64]{1,2,0:T(8,128)S(1)}, u32[]{:S(2)}, u32[]{:S(2)}) %all-to-all-start.2) | async-done | bytes 1736736 | tf_op jit(solution)/shard_map/all_to_all | solution.py:41
  161.3 0.1 reduce_sum.18
  161.4 0.0 copy-done
  161.4 0.3 convolution_bitcast_fusion
  161.7 0.1 copy.12
  161.8 0.2 reshape.25
  162.0 12.1 %all_to_all.26 = f32[32,1,1024]{2,1,0:T(1,128)S(1)} all-to-all(f32[32,1,1024]{2,1,0:T(1,128)S(1)} %reshape.25), channel_id=1, replica_groups=mesh['row'=8,'col_0'=4,'col_1'=8] {'col_0','col_1'}, dimensions={0} | all-to-all | bytes 262144 | tf_op jit(solution)/shard_map/all_to_all | solution.py:41
  174.2 1.0 broadcast_in_dim.2
  175.2 5.6 %all-to-all-start.3 = ((bf16[8,848,64]{1,2,0:T(8,128)(2,1)}), bf16[8,848,64]{1,2,0:T(8,128)(2,1)S(1)}, u32[]{:S(2)}, u32[]{:S(2)}) async-start(bf16[8,848,64]{1,2,0:T(8,128)(2,1)} %broadcast_in_dim.2), calls=%async_computation.3 | async-start | bytes 1835008 | tf_op jit(solution)/shard_map/all_to_all | solution.py:47
  180.8 0.5 broadcast.5
  181.3 0.9 reduce
  182.2 0.1 reshape.26
  182.3 0.6 reduce_sum.19
  183.0 11.4 %all-to-all-done.3 = bf16[8,848,64]{1,2,0:T(8,128)(2,1)S(1)} async-done(((bf16[8,848,64]{1,2,0:T(8,128)(2,1)}), bf16[8,848,64]{1,2,0:T(8,128)(2,1)S(1)}, u32[]{:S(2)}, u32[]{:S(2)}) %all-to-all-start.3) | async-done | bytes 868384 | tf_op jit(solution)/shard_map/all_to_all | solution.py:47
  194.4 1.8 convolution_convert_fusion
  (2 shorter events, 0.0 us)
Async XLA Ops:
  0.6 160.8 %copy-start = (bf16[848,512]{1,0:T(8,128)(2,1)S(1)}, bf16[848,512]{1,0:T(8,128)(2,1)}, u32[]{:S(2)}) copy-start(bf16[848,512]{1,0:T(8,128)(2,1)} %param.8) | copy-start | bytes 2605060
  0.6 24.5 %copy-start.1 = (s32[27136]{0:T(1024)S(1)}, s32[27136]{0:T(1024)}, u32[]{:S(2)}) copy-start(s32[27136]{0:T(1024)} %param.6) | copy-start | bytes 325636
  17.0 89.5 %all-to-all-start.1 = ((bf16[8,4,106,512]{3,1,2,0:T(4,128)(2,1)}), bf16[8,4,106,512]{3,1,2,0:T(4,128)(2,1)}, u32[]{:S(2)}, u32[]{:S(2)}) async-start(bf16[8,4,106,512]{3,1,2,0:T(4,128)(2,1)} %stack.7), calls=%async_computation.1 | async-start | bytes 6946816 | tf_op jit(solution)/shard_map/all_to_all | solution.py:21
  132.9 28.3 %all-to-all-start.2 = ((f32[8,848,64]{1,2,0:T(8,128)}), f32[8,848,64]{1,2,0:T(8,128)S(1)}, u32[]{:S(2)}, u32[]{:S(2)}) async-start(f32[8,848,64]{1,2,0:T(8,128)} %bitcast.17), calls=%async_computation.2 | async-start | bytes 3670016 | tf_op jit(solution)/shard_map/all_to_all | solution.py:41
  175.2 19.2 %all-to-all-start.3 = ((bf16[8,848,64]{1,2,0:T(8,128)(2,1)}), bf16[8,848,64]{1,2,0:T(8,128)(2,1)S(1)}, u32[]{:S(2)}, u32[]{:S(2)}) async-start(bf16[8,848,64]{1,2,0:T(8,128)(2,1)} %broadcast_in_dim.2), calls=%async_computation.3 | async-start | bytes 1835008 | tf_op jit(solution)/shard_map/all_to_all | solution.py:47
